TPU v7x, 8 devices: a whole 2x2x1 slice. The times are simulated.
8 devices in a mesh: dp: 2 (over z, y), tp: 4 (over x, core).
Axes of the slice: x: 2, y: 2, z: 1, core: 2. Of those that a mesh axis runs over, the one named last changes fastest.
Arguments:
- x_seq: bfloat16 [24, 512, 5120], P('dp', 'tp'), parts along dimension 0
- ln_gain: float32 [5120], replicated
- ln_bias: float32 [5120], replicated
- w_qkv: bfloat16 [5120, 40, 3, 128], P(None, 'tp')
- w_out: bfloat16 [5120, 5120], P('tp')
- w_up: bfloat16 [5120, 20480], P(None, 'tp')
- w_down: bfloat16 [20480, 5120], P('tp')
Outputs:
- output: bfloat16 [24, 512, 5120], P('dp', 'tp'), parts along dimension 0
There are 2 independent parts. A program takes and returns all parts, laid end to end along the dimension named above; an argument that names none is the same for every part.
All inputs are finite; a program needn't handle non-finite values.
Results may differ from a plain program's by a relative error of at most 0.00944055.
Values are sent between devices in bfloat16 or wider.
A program may use at most 1 GiB of HBM per device.

v0:
```python
import jax
import jax.numpy as jnp
from jax import lax
from jax.sharding import PartitionSpec as P, NamedSharding

LN_EPS = 1e-5


def layer_norm(x_f32, ln_gain, ln_bias):
    row_mean = jnp.mean(x_f32, axis=-1, keepdims=True)
    centered = x_f32 - row_mean
    variance = jnp.mean(centered * centered, axis=-1, keepdims=True)
    return centered * lax.rsqrt(variance + LN_EPS) * ln_gain + ln_bias


def solution(mesh):
    def local_layer(x_blk, ln_gain, ln_bias, w_qkv, w_out, w_up, w_down):
        x_full = lax.all_gather(x_blk, "tp", axis=1, tiled=True)
        seq_len = x_full.shape[1]
        model_dim = x_full.shape[2]
        kv_local, group_width, head_dim = w_qkv.shape[1:]
        group_q = group_width - 2
        normed = layer_norm(x_full.astype(jnp.float32), ln_gain, ln_bias).astype(jnp.bfloat16)
        proj_qkv = jnp.einsum("bsd,dgjh->bsgjh", normed, w_qkv,
                              preferred_element_type=jnp.float32).astype(jnp.bfloat16)
        queries = proj_qkv[:, :, :, :group_q]
        key_rows = proj_qkv[:, :, :, group_q]
        value_rows = proj_qkv[:, :, :, group_q + 1]
        scores = jnp.einsum("bsgjh,btgh->bgjst", queries, key_rows,
                            preferred_element_type=jnp.float32) * (head_dim ** -0.5)
        causal = (lax.broadcasted_iota(jnp.int32, (seq_len, seq_len), 0)
                  >= lax.broadcasted_iota(jnp.int32, (seq_len, seq_len), 1))
        scores = jnp.where(causal, scores, -jnp.inf)
        attn_prob = jax.nn.softmax(scores, axis=-1).astype(jnp.bfloat16)
        context = jnp.einsum("bgjst,btgh->bgjsh", attn_prob, value_rows,
                             preferred_element_type=jnp.float32).astype(jnp.bfloat16)
        w_heads = w_out.reshape(kv_local, group_q, head_dim, model_dim)
        attn_part = jnp.einsum("bgjsh,gjhd->bsd", context, w_heads, preferred_element_type=jnp.float32)
        hidden = jnp.einsum("bsd,df->bsf", normed, w_up, preferred_element_type=jnp.float32)
        activated = jax.nn.gelu(hidden, approximate=False).astype(jnp.bfloat16)
        mlp_part = jnp.einsum("bsf,fd->bsd", activated, w_down, preferred_element_type=jnp.float32)
        branch_part = (attn_part + mlp_part).astype(jnp.bfloat16)
        branch = lax.psum_scatter(branch_part, "tp", scatter_dimension=1, tiled=True)
        return (x_blk.astype(jnp.float32) + branch.astype(jnp.float32)).astype(jnp.bfloat16)

    return jax.shard_map(
        local_layer, mesh=mesh,
        in_specs=(P("dp", "tp", None), P(), P(), P(None, "tp", None, None),
                  P("tp", None), P(None, "tp"), P("tp", None)),
        out_specs=P("dp", "tp", None), check_vma=False)
```

profile of v0, /device:TPU:0, one launch (start us, length us, event | category | flops | bytes accessed | tf_op | source)
XLA Modules:
  0.0 2379.2 jit_solution(11337888551511831287)
XLA Ops:
  6.5 0.0 copy-start.5
  6.5 0.0 copy-start.7
  6.5 0.0 all-gather.2.cloned.1.call-start
  6.5 0.7 all-gather.2.cloned.1.call-update
  7.3 0.0 reduce-scatter.2.cloned.1.call-start
  7.3 0.8 iota_compare_fusion
  8.1 369.5 %all-gather.2.cloned.1.call-done = bf16[12,512,5120]{2,1,0:T(8,128)(2,1)} async-done(((bf16[12,128,5120]{2,1,0:T(8,128)(2,1)}), bf16[12,512,5120]{2,1,0:T(8,128)(2,1)}) %all-gather.2.cloned.1.call-update) | async-done | bytes 62914576 | tf_op jit(solution)/shard_map/all_gather | solution.py:18
  377.6 19.8 convert_reduce_fusion
  397.4 0.0 copy-start.1
  397.4 23.3 fusion.2
  420.7 0.0 copy-done.1
  420.7 0.0 copy-start.3
  420.7 0.6 copy-done.3
  421.3 0.0 copy-done.5
  421.3 0.0 copy-done.7
  421.3 0.0 copy-start
  421.3 276.7 %fusion.39 = bf16[12,512,10,3,128]{4,1,3,2,0:T(8,128)(2,1)} fusion(bf16[5120,10,3,128]{3,0,2,1:T(8,128)(2,1)} %param.10, f32[5120]{0:T(1024)S(1)} %copy-done.5, f32[5120]{0:T(1024)S(1)} %copy-done.7, f32[12,512]{1,0:T(8,128)S(1)} %add_rsqrt_fusion, f32[12,512]{1,0:T(8,128)S(1)} %broadcast_multiply_fusion, ...), kind=kOutput, calls=%fused_computation.52 | convolution fusion | flops 241804247040 | bytes 149512192 | tf_op jit(solution)/shard_map/bsd,dgjh->bsgjh/dot_general | solution.py:24
  698.0 0.0 copy-done
  698.0 53.6 %fusion.17 = (f32[12,10,512]{2,1,0:T(8,128)S(1)}, f32[12,10,512,512]{3,2,1,0:T(8,128)}) fusion(pred[512,512]{0,1:T(8,128)(4,1)S(1)} %copy-done, bf16[12,512,10,3,128]{4,1,3,2,0:T(8,128)(2,1)} %fusion.39), kind=kOutput, calls=%fused_computation.36 | convolution fusion | flops 8147374080 | bytes 157794304 | tf_op jit(solution)/shard_map/bsgjh,btgh->bgjst/dot_general | solution.py:29
  751.6 38.8 %fusion.16 = f32[12,10,512]{2,1,0:T(8,128)S(1)} fusion(f32[12,10,512,512]{3,2,1,0:T(8,128)} %get-tuple-element.8, f32[12,10,512]{2,1,0:T(8,128)S(1)} %get-tuple-element.7, pred[512,512]{0,1:T(8,128)(4,1)S(1)} %copy-done), kind=kLoop, calls=%fused_computation.35 | loop fusion | flops 125767680 | bytes 126582784 | tf_op jit(solution)/shard_map/reduce_sum | solution.py:34
  790.5 54.6 %fusion.101 = bf16[12,10,512,128]{3,2,1,0:T(8,128)(2,1)} fusion(bf16[12,512,10,3,128]{4,1,3,2,0:T(8,128)(2,1)} %fusion.39, f32[12,10,512]{2,1,0:T(8,128)S(1)} %fusion.16, f32[12,10,512]{2,1,0:T(8,128)S(1)} %get-tuple-element.7, f32[12,10,512,512]{3,2,1,0:T(8,128)} %get-tuple-element.8, pred[512,512]{0,1:T(8,128)(4,1)S(1)} %copy-done), kind=kOutput, calls=%fused_computation.58.clone.1 | convolution fusion | flops 8218214400 | bytes 158040064 | tf_op jit(solution)/shard_map/bgjst,btgh->bgjsh/dot_general | solution.py:35
  845.1 0.0 copy-start.2
  845.1 0.0 copy-start.4
  845.1 0.0 copy-start.6
  845.1 0.0 copy-start.8
  845.1 92.9 %fusion.45 = f32[12,512,5120,1]{2,1,3,0:T(8,128)} fusion(bf16[10,128,5120,1]{2,1,0,3:T(8,128)(2,1)} %bitcast.98, bf16[12,10,512,128]{3,2,1,0:T(8,128)(2,1)} %fusion.101), kind=kOutput, calls=%fused_computation.57 | convolution fusion | flops 80530636800 | bytes 154664960 | tf_op jit(solution)/shard_map/bgjsh,gjhd->bsd/dot_general | solution.py:38
  938.0 0.0 copy-done.2
  938.0 0.0 copy-done.4
  938.0 0.0 copy-done.6
  938.0 0.0 copy-done.8
  938.0 387.4 %fusion.23 = (u16[512,5120]{1,0:T(8,128)(2,1)}, u16[512,5120]{1,0:T(8,128)(2,1)}, f32[12,512,5120]{2,1,0:T(8,128)}) fusion(bf16[5120,5120]{1,0:T(8,128)(2,1)} %param.12, bf16[12,512,5120]{2,1,0:T(8,128)(2,1)} %all-gather.2.cloned.1.call-done, f32[5120]{0:T(1024)S(1)} %copy-done.6, f32[5120]{0:T(1024)S(1)} %copy-done.8, f32[12,512]{1,0:T(8,128)S(1)} %copy-done.4, ...), kind=kOutput, calls=%fused_computation.42 | convolution fusion | flops 322714992640 | bytes 251748352 | tf_op jit(solution)/shard_map/bsd,df->bsf/dot_general | solution.py:39
  1325.4 287.0 %fusion.98 = bf16[12,512,5120]{2,1,0:T(8,128)(2,1)} fusion(f32[12,512,5120]{2,1,0:T(8,128)} %get-tuple-element.9, u16[512,5120]{1,0:T(8,128)(2,1)} %get-tuple-element.6, u16[512,5120]{1,0:T(8,128)(2,1)} %get-tuple-element.5), kind=kLoop, calls=%fused_computation.11.clone.clone.clone.clone.1 | loop fusion | flops 2202009600 | bytes 199229440 | tf_op jit(solution)/shard_map/bsf,fd->bsd/dot_general | solution.py:41
  1612.5 340.1 %fusion.9 = bf16[12,512,5120]{2,1,0:T(8,128)(2,1)} fusion(f32[12,512,5120,1]{2,1,3,0:T(8,128)} %fusion.45, bf16[5120,5120]{1,0:T(8,128)(2,1)} %param.13, bf16[12,512,5120]{2,1,0:T(8,128)(2,1)} %fusion.98), kind=kOutput, calls=%fused_computation.19 | convolution fusion | flops 322185461760 | bytes 304087040 | tf_op jit(solution)/shard_map/bsf,fd->bsd/dot_general | solution.py:41
  1952.6 0.0 reduce-scatter.2.cloned.1.call-update
  1952.6 401.1 %reduce-scatter.2.cloned.1.call-done = bf16[12,128,5120]{2,1,0:T(8,128)(2,1)} async-done(((bf16[12,512,5120]{2,1,0:T(8,128)(2,1)}), bf16[12,128,5120]{2,1,0:T(8,128)(2,1)}) %reduce-scatter.2.cloned.1.call-update) | async-done | bytes 15728656 | tf_op jit(solution)/shard_map/reduce_scatter | solution.py:43
  2353.8 18.2 add_convert_fusion
  (2 shorter events, 0.0 us)
Async XLA Ops:
  6.5 414.8 %copy-start.5 = (f32[5120]{0:T(1024)S(1)}, f32[5120]{0:T(1024)}, u32[]{:S(2)}) copy-start(f32[5120]{0:T(1024)} %param.9) | copy-start | bytes 61444
  6.5 414.8 %copy-start.7 = (f32[5120]{0:T(1024)S(1)}, f32[5120]{0:T(1024)}, u32[]{:S(2)}) copy-start(f32[5120]{0:T(1024)} %param.8) | copy-start | bytes 61444
  6.5 371.0 %all-gather.2.cloned.1.call-start = ((), (), s32[]{:S(2)}) async-start(), calls=%async_computation.1 | async-start | bytes 78643200 | tf_op jit(solution)/shard_map/all_gather | solution.py:18
  7.3 2346.5 %reduce-scatter.2.cloned.1.call-start = ((), (), s32[]{:S(2)}) async-start(), calls=%async_computation.2 | async-start | bytes 78643200 | tf_op jit(solution)/shard_map/reduce_scatter | solution.py:43
  397.4 23.3 copy-start.1
  420.7 0.6 copy-start.3
  421.3 276.7 %copy-start = (pred[512,512]{0,1:T(8,128)(4,1)S(1)}, pred[512,512]{0,1:T(8,128)(4,1)}, u32[]{:S(2)}) copy-start(pred[512,512]{0,1:T(8,128)(4,1)} %iota_compare_fusion) | copy-start | bytes 786436
  845.1 92.9 %copy-start.2 = (f32[12,512]{1,0:T(8,128)S(1)}, f32[12,512]{1,0:T(8,128)}, u32[]{:S(2)}) copy-start(f32[12,512]{1,0:T(8,128)} %copy-done.1) | copy-start | bytes 73732
  845.1 92.9 %copy-start.4 = (f32[12,512]{1,0:T(8,128)S(1)}, f32[12,512]{1,0:T(8,128)}, u32[]{:S(2)}) copy-start(f32[12,512]{1,0:T(8,128)} %copy-done.3) | copy-start | bytes 73732
  845.1 92.9 %copy-start.6 = (f32[5120]{0:T(1024)S(1)}, f32[5120]{0:T(1024)}, u32[]{:S(2)}) copy-start(f32[5120]{0:T(1024)} %param.9) | copy-start | bytes 61444
  845.1 92.9 %copy-start.8 = (f32[5120]{0:T(1024)S(1)}, f32[5120]{0:T(1024)}, u32[]{:S(2)}) copy-start(f32[5120]{0:T(1024)} %param.8) | copy-start | bytes 61444
Sparse Core Ops, SparseCore 0:
  8.9 368.6 all-gather.1
  1952.7 400.9 reduce-scatter.1
where the time goes:
time: 2390 us; the launch traced here: 2380 us
  matrix products  1210 us (51%)
  waiting for transfers between devices  771 us (32%)
  other arithmetic  388 us (16%)
    reduce_scatter x1, waiting for transfers between devices, local_layer(): lax.psum_scatter(branch_part, 'tp', scatter_dimension=1, tiled=True)  401 us
    dot_general x1, matrix products, local_layer(): jnp.einsum('bsd,df->bsf', normed, w_up, preferred_element_type=jnp.float32)  387 us
    all_gather x1, waiting for transfers between devices, local_layer(): x_full = lax.all_gather(x_blk, 'tp', axis=1, tiled=True)  369 us
    dot_general x1, matrix products, local_layer(): jnp.einsum('bsf,fd->bsd', activated, w_down, preferred_element_type=jnp.f...  340 us
    dot_general x1, other arithmetic, local_layer(): jnp.einsum('bsf,fd->bsd', activated, w_down, preferred_element_type=jnp.f...  287 us
    dot_general x1, matrix products, local_layer(): jnp.einsum('bsd,dgjh->bsgjh', normed, w_qkv, preferred_element_type=jnp.f...  277 us
    dot_general x1, matrix products, local_layer(): jnp.einsum('bgjsh,gjhd->bsd', context, w_heads, preferred_element_type=jn...  92.9 us
    dot_general x1, matrix products, local_layer(): jnp.einsum('bgjst,btgh->bgjsh', attn_prob, value_rows, preferred_element_...  54.6 us
  transfers between devices with their start and end apart: 2, of which 2 were waited for; matrix products, arithmetic and copies ran while one was open for 0% of the time, Pallas kernels for 0%

commit v1 on v0

v1 whole, which is shorter than its diff:
```python
import functools

import jax
import jax.numpy as jnp
from jax import lax
from jax.experimental import pallas as pl
from jax.experimental.pallas import tpu as pltpu
from jax.sharding import PartitionSpec as P

LN_EPS = 1e-5
BF = jnp.bfloat16
F32 = jnp.float32
MESH = pl.DeviceIdType.MESH
ANY = pl.BlockSpec(memory_space=pl.ANY)
VMEM_LIMIT = 66_000_000


def ds(i, n):
    return pl.ds(pl.multiple_of(i * n, n), n)


def neighbours():
    t = lax.axis_index("tp")
    c = t % 2
    sib = t + 1 - 2 * c
    far = (t + 2) % 4
    far_sib = (sib + 2) % 4
    return t, sib, far, far_sib


def meet(sib, far):
    barrier = pltpu.get_barrier_semaphore()
    for peer in (sib, far):
        pl.semaphore_signal(barrier, inc=1, device_id={"tp": peer}, device_id_type=MESH)
    pl.semaphore_wait(barrier, 2)


def send(src, dst, send_sem, recv_sem, peer):
    return pltpu.make_async_remote_copy(src_ref=src, dst_ref=dst, send_sem=send_sem, recv_sem=recv_sem,
                                        device_id={"tp": peer}, device_id_type=MESH)


def ln_body(x_ref, g_ref, b_ref, o_ref):
    x = x_ref[...].astype(F32)
    mean = jnp.mean(x, axis=-1, keepdims=True)
    cen = x - mean
    var = jnp.mean(cen * cen, axis=-1, keepdims=True)
    o_ref[...] = (cen * lax.rsqrt(var + LN_EPS) * g_ref[...] + b_ref[...]).astype(BF)


def ln_call(x, gain, bias, rows=128):
    m, d = x.shape
    return pl.pallas_call(
        ln_body, grid=(m // rows,),
        in_specs=[pl.BlockSpec((rows, d), lambda i: (i, 0)), pl.BlockSpec((1, d), lambda i: (0, 0)),
                  pl.BlockSpec((1, d), lambda i: (0, 0))],
        out_specs=pl.BlockSpec((rows, d), lambda i: (i, 0)),
        out_shape=jax.ShapeDtypeStruct((m, d), BF),
        compiler_params=pltpu.CompilerParams(vmem_limit_bytes=VMEM_LIMIT), name="ln")(x, gain, bias)


def enter_body(n_ref, wq_ref, wu_ref, qkv_ref, h_ref, in_ref, lhs, wq, wu, oq, ou,
               lhs_sem, wq_sem, wu_sem, oq_sem, ou_sem, ssem, rsem, *, M, TQ, TU, NQ, NU):
    t, sib, far, far_sib = neighbours()
    meet(sib, far)
    half = n_ref.shape[0] // 2
    heads = TQ // 384

    def part(ref, k):
        return ref.at[pl.ds(k * half, half), :]

    far_cp = [send(part(n_ref, k), in_ref.at[1, pl.ds(k * half, half), :], ssem.at[k], rsem.at[k], far) for k in (0, 1)]
    sib_cp = [send(part(n_ref, k), in_ref.at[0, pl.ds(k * half, half), :], ssem.at[2 + k], rsem.at[2 + k], sib)
              for k in (0, 1)]
    fwd_cp = [send(in_ref.at[1, pl.ds(k * half, half), :], in_ref.at[2, pl.ds(k * half, half), :], ssem.at[4 + k],
                   rsem.at[4 + k], sib) for k in (0, 1)]

    def wq_copies(j, slot):
        return [pltpu.make_async_copy(wq_ref.at[j * heads + i, k], wq.at[slot, :, pl.ds((i * 3 + k) * 128, 128)],
                                      wq_sem.at[slot, i * 3 + k]) for i in range(heads) for k in range(3)]

    def wu_copy(j, slot):
        return pltpu.make_async_copy(wu_ref.at[:, ds(j, TU)], wu.at[slot], wu_sem.at[slot])

    def own_lhs(k, slot):
        return pltpu.make_async_copy(n_ref.at[ds(k, M), :], lhs.at[slot], lhs_sem.at[slot])

    def in_lhs(which, k, slot):
        return pltpu.make_async_copy(in_ref.at[which, ds(k, M), :], lhs.at[slot], lhs_sem.at[slot])

    for cp in (far_cp[0], sib_cp[0], sib_cp[1], far_cp[1]):
        cp.start()
    own_lhs(0, 0).start()
    for cp in wq_copies(0, 0):
        cp.start()

    def block(b, _):
        ls = lax.rem(b, 2)
        k = jnp.where(b < 4, lax.rem(b, 2), (b - 4) // 2)
        which = jnp.where(b < 4, b // 2, 2 + lax.rem(b, 2))
        pos = jnp.where(which == 0, t, jnp.where(which == 1, sib, jnp.where(which == 2, far, far_sib)))
        pltpu.make_async_copy(n_ref.at[pl.ds(0, M), :], lhs.at[ls], lhs_sem.at[ls]).wait()

        def q_step(j, _):
            g = b * NQ + j
            slot = lax.rem(g, 2)
            for cp in wq_copies(j, slot):
                cp.wait()

            @pl.when(j < NQ - 1)
            def _():
                for cp in wq_copies(j + 1, 1 - slot):
                    cp.start()

            @pl.when(j == NQ - 1)
            def _():
                wu_copy(0, 0).start()

            @pl.when(g >= 2)
            def _():
                pltpu.make_async_copy(oq.at[slot], qkv_ref.at[0, pl.ds(0, M), pl.ds(0, TQ)], oq_sem.at[slot]).wait()
            oq[slot] = jnp.dot(lhs[ls], wq[slot], preferred_element_type=F32).astype(BF)
            pltpu.make_async_copy(oq.at[slot], qkv_ref.at[pos, ds(k, M), ds(j, TQ)], oq_sem.at[slot]).start()
            return 0

        lax.fori_loop(0, NQ, q_step, 0)

        def u_step(j, _):
            slot = lax.rem(j, 2)
            wu_copy(j, slot).wait()

            @pl.when(j < NU - 1)
            def _():
                wu_copy(j + 1, 1 - slot).start()

            @pl.when((j == NU - 1) & (b < 7))
            def _():
                for cp in wq_copies(0, lax.rem((b + 1) * NQ, 2)):
                    cp.start()

            @pl.when(j == NU // 2)
            def _():
                nxt = 1 - ls

                @pl.when(b == 0)
                def _():
                    own_lhs(1, nxt).start()

                for bb, kk in ((1, 0), (2, 1)):
                    @pl.when(b == bb)
                    def _():
                        sib_cp[kk].wait_recv()
                        in_lhs(0, kk, nxt).start()

                for bb, kk in ((3, 0), (5, 1)):
                    @pl.when(b == bb)
                    def _():
                        far_cp[kk].wait_recv()
                        fwd_cp[kk].start()
                        in_lhs(1, kk, nxt).start()

                for bb, kk in ((4, 0), (6, 1)):
                    @pl.when(b == bb)
                    def _():
                        fwd_cp[kk].wait_recv()
                        in_lhs(2, kk, nxt).start()

            @pl.when((b > 0) | (j >= 2))
            def _():
                pltpu.make_async_copy(ou.at[slot], h_ref.at[0, pl.ds(0, M), pl.ds(0, TU)], ou_sem.at[slot]).wait()
            z = jnp.dot(lhs[ls], wu[slot], preferred_element_type=F32)
            ou[slot] = (z * 0.5 * (1.0 + lax.erf(z * 0.7071067811865476))).astype(BF)
            pltpu.make_async_copy(ou.at[slot], h_ref.at[which, ds(k, M), ds(j, TU)], ou_sem.at[slot]).start()
            return 0

        lax.fori_loop(0, NU, u_step, 0)
        return 0

    lax.fori_loop(0, 8, block, 0)
    for s in (0, 1):
        pltpu.make_async_copy(oq.at[s], qkv_ref.at[0, pl.ds(0, M), pl.ds(0, TQ)], oq_sem.at[s]).wait()
        pltpu.make_async_copy(ou.at[s], h_ref.at[0, pl.ds(0, M), pl.ds(0, TU)], ou_sem.at[s]).wait()
    for cp in far_cp + sib_cp + fwd_cp:
        cp.wait_send()


def enter_call(n, wq, wu):
    rows, d = n.shape
    M, TQ, TU = rows // 2, 768, 512
    cq, cu = wq.shape[0] * 384, wu.shape[1]
    NQ, NU = cq // TQ, cu // TU
    return pl.pallas_call(
        functools.partial(enter_body, M=M, TQ=TQ, TU=TU, NQ=NQ, NU=NU),
        in_specs=[ANY] * 3, out_specs=[ANY] * 3,
        out_shape=[jax.ShapeDtypeStruct((4, rows, cq), BF), jax.ShapeDtypeStruct((4, rows, cu), BF),
                   jax.ShapeDtypeStruct((3, rows, d), BF)],
        scratch_shapes=[pltpu.VMEM((2, M, d), BF), pltpu.VMEM((2, d, TQ), BF), pltpu.VMEM((2, d, TU), BF),
                        pltpu.VMEM((2, M, TQ), BF), pltpu.VMEM((2, M, TU), BF),
                        pltpu.SemaphoreType.DMA((2,)), pltpu.SemaphoreType.DMA((2, TQ // 128)),
                        pltpu.SemaphoreType.DMA((2,)), pltpu.SemaphoreType.DMA((2,)), pltpu.SemaphoreType.DMA((2,)),
                        pltpu.SemaphoreType.DMA((6,)), pltpu.SemaphoreType.DMA((6,))],
        compiler_params=pltpu.CompilerParams(collective_id=0, has_side_effects=True, vmem_limit_bytes=VMEM_LIMIT),
        name="enter")(n, wq, wu)


def attend_body(qkv_ref, o_ref, *, heads, scale):
    Q = 256
    c = scale * 1.4426950408889634
    keep = (lax.broadcasted_iota(jnp.int32, (Q, Q), 0) >= lax.broadcasted_iota(jnp.int32, (Q, Q), 1))

    def probs(s):
        m = jnp.max(s, axis=-1, keepdims=True)
        p = jnp.exp2((s - m) * c)
        return (p * (1.0 / jnp.sum(p, axis=-1, keepdims=True))).astype(BF)

    def head(g):
        def grab(i, j):
            col = pl.ds(pl.multiple_of(g * 384 + j * 128, 128), 128)
            return qkv_ref[2 * i:2 * i + 2, 0, :, col].reshape(Q, 128)
        q = [grab(i, 0) for i in (0, 1)]
        k = [grab(i, 1) for i in (0, 1)]
        v = [grab(i, 2) for i in (0, 1)]
        dn = (((1,), (1,)), ((), ()))
        s00 = lax.dot_general(q[0], k[0], dn, preferred_element_type=F32)
        s10 = lax.dot_general(q[1], k[0], dn, preferred_element_type=F32)
        s11 = lax.dot_general(q[1], k[1], dn, preferred_element_type=F32)
        p0 = probs(jnp.where(keep, s00, -jnp.inf))
        p1 = probs(jnp.concatenate([s10, jnp.where(keep, s11, -jnp.inf)], axis=1))
        o0 = jnp.dot(p0, v[0], preferred_element_type=F32)
        o1 = jnp.dot(p1, jnp.concatenate(v, axis=0), preferred_element_type=F32)
        col = pl.ds(pl.multiple_of(g * 128, 128), 128)
        o_ref[0:2, 0, :, col] = o0.astype(BF).reshape(2, 128, 128)
        o_ref[2:4, 0, :, col] = o1.astype(BF).reshape(2, 128, 128)

    @pl.loop(0, heads // 2)
    def _(i):
        head(2 * i)
        head(2 * i + 1)


def attend_call(qkv, heads):
    _, b, s, cq = qkv.shape
    return pl.pallas_call(
        functools.partial(attend_body, heads=heads, scale=128 ** -0.5), grid=(b,),
        in_specs=[pl.BlockSpec((4, 1, s, cq), lambda i: (0, i, 0, 0))],
        out_specs=pl.BlockSpec((4, 1, s, heads * 128), lambda i: (0, i, 0, 0)),
        out_shape=jax.ShapeDtypeStruct((4, b, s, heads * 128), BF),
        compiler_params=pltpu.CompilerParams(vmem_limit_bytes=VMEM_LIMIT), name="attend")(qkv)


def leave_body(c_ref, h_ref, wo_ref, wd_ref, x_ref, y_ref, out_d2d, out_ici, in_ro, in_sib, in_ici,
               lc, lh, wo, wd, stage, ra, rb, xs,
               lc_sem, lh_sem, wo_sem, wd_sem, st_sem, ra_sem, rb_sem, xs_sem,
               s_ro, r_ro, s_sib, r_sib, s_ici, r_ici, *, M, T, N):
    t, sib, far, far_sib = neighbours()
    meet(sib, far)

    def w_copies(j, slot):
        return (pltpu.make_async_copy(wo_ref.at[:, ds(j, T)], wo.at[slot], wo_sem.at[slot]),
                pltpu.make_async_copy(wd_ref.at[:, ds(j, T)], wd.at[slot], wd_sem.at[slot]))

    def l_copies(pos, rel, k, slot):
        return (pltpu.make_async_copy(c_ref.at[pos, ds(k, M), :], lc.at[slot], lc_sem.at[slot]),
                pltpu.make_async_copy(h_ref.at[rel, ds(k, M), :], lh.at[slot], lh_sem.at[slot]))

    def start(cps):
        for cp in cps:
            cp.start()

    def ro_send(k, j):
        return send(out_d2d.at[0, k, j], in_ro.at[k, j], s_ro.at[k, j], r_ro.at[k, j], sib)

    def sib_send(k, j):
        return send(out_d2d.at[1, k, j], in_sib.at[k, j], s_sib.at[k, j], r_sib.at[k, j], sib)

    def ici_send(k, j):
        return send(out_ici.at[k, j], in_ici.at[k, j], s_ici.at[k, j], r_ici.at[k, j], far)

    def put(kind, k, j, slot):
        if kind == "own":
            dst = y_ref.at[ds(k, M), ds(j, T)]
        elif kind == "rs":
            dst = out_ici.at[k, j]
        else:
            dst = out_d2d.at[0 if kind == "ro" else 1, k, j]
        return pltpu.make_async_copy(stage.at[slot], dst, st_sem.at[slot])

    remote = {"ro": ro_send, "rs": ici_send, "sib": sib_send}
    rel_of = {"own": 0, "sib": 1, "rs": 2, "ro": 3}
    pos_of = {"own": t, "sib": sib, "rs": far, "ro": far_sib}

    def adds(kind, k, j, slot):
        if kind == "rs":
            ro_send(k, j).wait_recv()
            pltpu.make_async_copy(in_ro.at[k, j], ra.at[slot], ra_sem.at[slot]).start()
        if kind == "own":
            sib_send(k, j).wait_recv()
            ici_send(k, j).wait_recv()
            pltpu.make_async_copy(in_sib.at[k, j], ra.at[slot], ra_sem.at[slot]).start()
            pltpu.make_async_copy(in_ici.at[k, j], rb.at[slot], rb_sem.at[slot]).start()
            pltpu.make_async_copy(x_ref.at[ds(k, M), ds(j, T)], xs.at[slot], xs_sem.at[slot]).start()

    def run(kind, k, ls, nxt, prev):
        for cp in l_copies(0, 0, 0, ls):
            cp.wait()

        def step(j, _):
            slot = lax.rem(j, 2)
            for cp in w_copies(j, slot):
                cp.wait()

            @pl.when(j < N - 1)
            def _():
                start(w_copies(j + 1, 1 - slot))
                adds(kind, k, j + 1, 1 - slot)

            if nxt is not None:
                for nk, nh, cond in nxt:
                    @pl.when((j == N - 1) & cond)
                    def _():
                        start(w_copies(0, 0))
                        adds(nk, nh, 0, 0)

                    @pl.when((j == N // 2) & cond)
                    def _():
                        start(l_copies(pos_of[nk], rel_of[nk], nh, 1 - ls))

            if kind in ("rs", "own"):
                pltpu.make_async_copy(in_ro.at[0, 0], ra.at[slot], ra_sem.at[slot]).wait()
            if kind == "own":
                pltpu.make_async_copy(in_ici.at[0, 0], rb.at[slot], rb_sem.at[slot]).wait()
                pltpu.make_async_copy(x_ref.at[pl.ds(0, M), pl.ds(0, T)], xs.at[slot], xs_sem.at[slot]).wait()
            z = (jnp.dot(lc[ls], wo[slot], preferred_element_type=F32)
                 + jnp.dot(lh[ls], wd[slot], preferred_element_type=F32))
            if kind == "rs":
                z = z + ra[slot].astype(F32)
            if kind == "own":
                z = (z + ra[slot].astype(F32)) + rb[slot].astype(F32)
                z = xs[slot].astype(F32) + z.astype(BF).astype(F32)
            stage[slot] = z.astype(BF)

            @pl.when(j > 0)
            def _():
                put(kind, k, j - 1, 1 - slot).wait()
                if kind != "own":
                    remote[kind](k, j - 1).start()

            for pk, ph, cond in prev:
                @pl.when((j == 0) & cond)
                def _():
                    put(pk, ph, N - 1, 1).wait()
                    if pk != "own":
                        remote[pk](ph, N - 1).start()
            put(kind, k, j, slot).start()
            return 0

        lax.fori_loop(0, N, step, 0)

    start(w_copies(0, 0))
    start(l_copies(pos_of["ro"], rel_of["ro"], 0, 0))

    def pair(p, _):
        run("ro", p, 0, [("rs", p, p >= 0)], [("rs", p - 1, p > 0)])
        run("rs", p, 1, [("ro", p + 1, p == 0), ("sib", 0, p == 1)], [("ro", p, p >= 0)])
        return 0

    lax.fori_loop(0, 2, pair, 0)

    def sib_pair(p, _):
        run("sib", p, lax.rem(p, 2), [("sib", p + 1, p == 0), ("own", 0, p == 1)], [("rs", 1, p == 0), ("sib", p - 1, p > 0)])
        return 0

    lax.fori_loop(0, 2, sib_pair, 0)

    def own_pair(p, _):
        run("own", p, lax.rem(p, 2), [("own", p + 1, p == 0)], [("sib", 1, p == 0), ("own", p - 1, p > 0)])
        return 0

    lax.fori_loop(0, 2, own_pair, 0)
    put("own", 1, N - 1, 1).wait()

    def drain(i, _):
        k, j = i // N, lax.rem(i, N)
        ro_send(k, j).wait_send()
        sib_send(k, j).wait_send()
        ici_send(k, j).wait_send()
        return 0

    lax.fori_loop(0, 2 * N, drain, 0)


def leave_call(ctx, h, wo, wd, x):
    rows, d = x.shape
    M, T = rows // 2, 512
    N = d // T
    kc, kh = ctx.shape[2], h.shape[2]
    tile = (2, N, M, T)
    dma = pltpu.SemaphoreType.DMA
    out = pl.pallas_call(
        functools.partial(leave_body, M=M, T=T, N=N),
        in_specs=[ANY] * 5, out_specs=[ANY] * 6,
        out_shape=[jax.ShapeDtypeStruct((rows, d), BF), jax.ShapeDtypeStruct((2,) + tile, BF)]
        + [jax.ShapeDtypeStruct(tile, BF)] * 4,
        scratch_shapes=[pltpu.VMEM((2, M, kc), BF), pltpu.VMEM((2, M, kh), BF), pltpu.VMEM((2, kc, T), BF),
                        pltpu.VMEM((2, kh, T), BF)] + [pltpu.VMEM((2, M, T), BF)] * 4
        + [dma((2,))] * 8 + [dma((2, N))] * 6,
        compiler_params=pltpu.CompilerParams(collective_id=1, has_side_effects=True, vmem_limit_bytes=VMEM_LIMIT),
        name="leave")(ctx, h, wo, wd, x)
    return out[0]


def solution(mesh):
    def local_layer(x_blk, ln_gain, ln_bias, w_qkv, w_out, w_up, w_down):
        b, s, d = x_blk.shape
        heads = w_qkv.shape[1]
        x = x_blk.reshape(b * s, d)
        n = ln_call(x, ln_gain.reshape(1, d), ln_bias.reshape(1, d))
        qkv, h, _ = enter_call(n, w_qkv.transpose(1, 2, 0, 3), w_up)
        ctx = attend_call(qkv.reshape(4, b, s, -1), heads)
        y = leave_call(ctx.reshape(4, b * s, -1), h, w_out, w_down, x)
        return y.reshape(b, s, d)

    return jax.shard_map(
        local_layer, mesh=mesh,
        in_specs=(P("dp", "tp", None), P(), P(), P(None, "tp", None, None),
                  P("tp", None), P(None, "tp"), P("tp", None)),
        out_specs=P("dp", "tp", None), check_vma=False)
```

time: 2390 us -> 1150 us (0.48)
  matrix products: 1210 us -> 0 us
  Pallas kernels: 0 us -> 1140 us
  waiting for transfers between devices: 771 us -> 0 us
  other arithmetic: 388 us -> 0 us
    dot_general x6 -> x0, matrix products: 1210 us -> none  [the longest x1 387 us: local_layer(): jnp.einsum('bsd,df->bsf', normed, w_up, preferred_element_type=jnp.float32)]
    pallas_call x0 -> x4, Pallas kernels: none -> 1140 us  [the longest x1 610 us: enter_call(): pl.pallas_call(functools.partial(enter_body, M=M, TQ=TQ, TU=TU, NQ=NQ, NU...]
    reduce_scatter x1 -> x0, waiting for transfers between devices: 401 us -> none  [local_layer(): lax.psum_scatter(branch_part, 'tp', scatter_dimension=1, tiled=True)]
    all_gather x1 -> x0, waiting for transfers between devices: 369 us -> none  [local_layer(): x_full = lax.all_gather(x_blk, 'tp', axis=1, tiled=True)]
    dot_general x1 -> x0, other arithmetic: 287 us -> none  [local_layer(): jnp.einsum('bsf,fd->bsd', activated, w_down, preferred_element_type=jnp.f...]
    reduce_sum x3 -> x0, other arithmetic: 81.9 us -> none  [the longest x1 38.8 us: local_layer(): attn_prob = jax.nn.softmax(scores, axis=-1).astype(jnp.bfloat16)]
  transfers between devices with their start and end apart: 2 -> 0, of which waited for: 2 -> 0; matrix products, arithmetic and copies ran while one was open for 0% -> 0% of each run, Pallas kernels for 0% -> 0%
where the time goes in v1:
time: 1150 us
  Pallas kernels  1140 us (99%)
  local copies, waits for them, and re-layouts  13.2 us (1%)
    pallas_call x1, Pallas kernels, enter_call(): pl.pallas_call(functools.partial(enter_body, M=M, TQ=TQ, TU=TU, NQ=NQ, NU...  610 us
    pallas_call x1, Pallas kernels, leave_call(): pl.pallas_call(functools.partial(leave_body, M=M, T=T, N=N), in_specs=[AN...  435 us
    pallas_call x1, Pallas kernels, attend_call(): pl.pallas_call(functools.partial(attend_body, heads=heads, scale=128 ** (...  74.4 us

profile of v1, /device:TPU:0, one launch (start us, length us, event | category | flops | bytes accessed | tf_op | source)
XLA Modules:
  0.0 1153.8 jit_solution(9934919152484145423)
XLA Ops:
  0.0 21.1 %ln.1.n_ref = bf16[1536,5120]{1,0:T(8,128)(2,1)} custom-call(bf16[1536,5120]{1,0:T(8,128)(2,1)} %bitcast.7, f32[1,5120]{1,0:T(1,128)} %bitcast.13, f32[1,5120]{1,0:T(1,128)} %bitcast.14), custom_call_target="tpu_custom_call" | custom-call | tf_op jit(solution)/shard_map/ln/pallas_call | solution.py:53
  21.1 609.8 %enter.1 = (bf16[4,1536,3840]{2,1,0:T(8,128)(2,1)}, bf16[4,1536,5120]{2,1,0:T(8,128)(2,1)}, bf16[3,1536,5120]{2,1,0:T(8,128)(2,1)}) custom-call(bf16[1536,5120]{1,0:T(8,128)(2,1)} %ln.1.n_ref, bf16[10,3,5120,128]{3,2,1,0:T(8,128)(2,1)} %bitcast.11, bf16[5120,5120]{1,0:T(8,128)(2,1)} %wu_ref.1), custom_call_target="tpu_custom_call" | custom-call | tf_op jit(solution)/shard_map/enter/pallas_call | solution.py:192
  630.9 74.4 %attend.1 = bf16[4,12,128,1280]{3,2,1,0:T(8,128)(2,1)} custom-call(bf16[4,12,128,3840]{3,2,1,0:T(8,128)(2,1)} %bitcast.10), custom_call_target="tpu_custom_call" | custom-call | tf_op jit(solution)/shard_map/attend/pallas_call | solution.py:243
  705.3 435.2 %leave.1 = (bf16[1536,5120]{1,0:T(8,128)(2,1)}, bf16[2,2,10,768,512]{4,3,2,1,0:T(8,128)(2,1)}, bf16[2,10,768,512]{3,2,1,0:T(8,128)(2,1)}, bf16[2,10,768,512]{3,2...) custom-call(bf16[4,1536,1280]{2,1,0:T(8,128)(2,1)} %bitcast.9, ...), custom_call_target="tpu_custom_call" | custom-call | tf_op jit(solution)/shard_map/leave/pallas_call | solution.py:399
  1140.5 13.2 %copy.9 = bf16[12,128,5120]{2,1,0:T(8,128)(2,1)} copy(bf16[12,128,5120]{2,1,0:T(8,128)(2,1)} %bitcast.12) | data formatting | bytes 31457280

commit v2 on v0

v2 whole, which is shorter than its diff:
```python
import functools

import jax
import jax.numpy as jnp
from jax import lax
from jax.experimental import pallas as pl
from jax.experimental.pallas import tpu as pltpu
from jax.sharding import PartitionSpec as P

LN_EPS = 1e-5
BF = jnp.bfloat16
F32 = jnp.float32
MESH = pl.DeviceIdType.MESH
ANY = pl.BlockSpec(memory_space=pl.ANY)
VMEM_LIMIT = 66_000_000


def ds(i, n):
    return pl.ds(pl.multiple_of(i * n, n), n)


def neighbours():
    t = lax.axis_index("tp")
    c = t % 2
    sib = t + 1 - 2 * c
    far = (t + 2) % 4
    far_sib = (sib + 2) % 4
    return t, sib, far, far_sib


def meet(sib, far):
    barrier = pltpu.get_barrier_semaphore()
    for peer in (sib, far):
        pl.semaphore_signal(barrier, inc=1, device_id={"tp": peer}, device_id_type=MESH)
    pl.semaphore_wait(barrier, 2)


def send(src, dst, send_sem, recv_sem, peer):
    return pltpu.make_async_remote_copy(src_ref=src, dst_ref=dst, send_sem=send_sem, recv_sem=recv_sem,
                                        device_id={"tp": peer}, device_id_type=MESH)


def enter_body(x_ref, g_ref, b_ref, wq_ref, wu_ref, qkv_ref, h_ref, n_ref, in_ref, lhs, w, o, xb,
               lhs_sem, w_sem, o_sem, x_sem, n_sem, ssem, rsem, *, M, T, NQ, NU):
    t, sib, far, far_sib = neighbours()
    steps = NQ + NU
    R, G = xb.shape[1], 16
    d = x_ref.shape[1]

    def half(ref, k):
        return ref.at[pl.ds(k * M, M), :]

    far_cp = [send(half(n_ref, k), half(in_ref.at[1], k), ssem.at[k], rsem.at[k], far) for k in (0, 1)]
    sib_cp = [send(half(n_ref, k), half(in_ref.at[0], k), ssem.at[2 + k], rsem.at[2 + k], sib) for k in (0, 1)]
    fwd_cp = [send(half(in_ref.at[1], k), half(in_ref.at[2], k), ssem.at[4 + k], rsem.at[4 + k], sib) for k in (0, 1)]

    def start_wq(j, slot):
        for i in range(T // 128):
            pltpu.make_async_copy(wq_ref.at[j * (T // 128) + i], w.at[slot, :, pl.ds(i * 128, 128)], w_sem.at[slot]).start()

    def wu_copy(j, slot):
        return pltpu.make_async_copy(wu_ref.at[:, ds(j, T)], w.at[slot], w_sem.at[slot])

    def in_lhs(which, k, slot):
        return pltpu.make_async_copy(in_ref.at[which, ds(k, M), :], lhs.at[slot], lhs_sem.at[slot])

    def x_copy(i, slot):
        return pltpu.make_async_copy(x_ref.at[ds(i, R), :], xb.at[slot], x_sem.at[slot])

    def n_copy(i):
        k, r = i // (M // R), lax.rem(i, M // R)
        return pltpu.make_async_copy(lhs.at[k, ds(r, R), :], n_ref.at[ds(i, R), :], n_sem.at[k])

    def leave_home(k):
        pltpu.make_async_copy(lhs.at[k], half(n_ref, k), n_sem.at[k]).wait()
        far_cp[k].start()
        sib_cp[k].start()

    x_copy(0, 0).start()
    start_wq(0, 0)
    meet(sib, far)

    def normalize(i, _):
        slot = lax.rem(i, 2)
        x_copy(i, slot).wait()

        @pl.when(i < 2 * M // R - 1)
        def _():
            x_copy(i + 1, 1 - slot).start()

        def rows(g, _):
            for u in range(2):
                r = pl.multiple_of((2 * g + u) * G, G)
                v = xb[slot, pl.ds(r, G), :].astype(F32)
                v = v - jnp.sum(v, axis=-1, keepdims=True) * (1.0 / d)
                rstd = lax.rsqrt(jnp.sum(v * v, axis=-1, keepdims=True) * (1.0 / d) + LN_EPS)
                lhs[i // (M // R), pl.ds(pl.multiple_of(lax.rem(i, M // R) * R + r, G), G), :] = (
                    v * rstd * g_ref[...] + b_ref[...]).astype(BF)
            return 0

        lax.fori_loop(0, R // (2 * G), rows, 0)
        n_copy(i).start()

        @pl.when(i == M // R)
        def _():
            leave_home(0)
        return 0

    lax.fori_loop(0, 2 * M // R, normalize, 0)

    def block(b, _):
        ls = lax.rem(b, 2)
        k = jnp.where(b < 4, lax.rem(b, 2), (b - 4) // 2)
        which = jnp.where(b < 4, b // 2, 2 + lax.rem(b, 2))
        pos = jnp.where(which == 0, t, jnp.where(which == 1, sib, jnp.where(which == 2, far, far_sib)))

        @pl.when(b >= 2)
        def _():
            in_lhs(0, 0, ls).wait()

        def begin(j, slot):
            wu_copy(0, slot).wait()

            @pl.when(j < NQ - 1)
            def _():
                start_wq(j + 1, 1 - slot)

            @pl.when((j >= NQ - 1) & (j < steps - 1))
            def _():
                wu_copy(j + 1 - NQ, 1 - slot).start()

            @pl.when((j == steps - 1) & (b < 7))
            def _():
                start_wq(0, 1 - slot)

            @pl.when((b > 0) | (j >= 2))
            def _():
                pltpu.make_async_copy(o.at[slot], h_ref.at[0, pl.ds(0, M), pl.ds(0, T)], o_sem.at[slot]).wait()

        def q_step(j, _):
            slot = lax.rem(b * steps + j, 2)
            begin(j, slot)

            @pl.when((b == 0) & (j == 1))
            def _():
                leave_home(1)
            o[slot] = jnp.dot(lhs[ls], w[slot], preferred_element_type=F32).astype(BF)
            pltpu.make_async_copy(o.at[slot], qkv_ref.at[pos, ds(k, M), ds(j, T)], o_sem.at[slot]).start()
            return 0

        lax.fori_loop(0, NQ, q_step, 0)

        def u_step(j, _):
            slot = lax.rem(b * steps + NQ + j, 2)
            begin(NQ + j, slot)

            @pl.when(j == NU // 2)
            def _():
                nxt = 1 - ls

                for bb, kk in ((1, 0), (2, 1)):
                    @pl.when(b == bb)
                    def _():
                        sib_cp[kk].wait_recv()
                        in_lhs(0, kk, nxt).start()

                for bb, kk in ((3, 0), (5, 1)):
                    @pl.when(b == bb)
                    def _():
                        far_cp[kk].wait_recv()
                        fwd_cp[kk].start()
                        in_lhs(1, kk, nxt).start()

                for bb, kk in ((4, 0), (6, 1)):
                    @pl.when(b == bb)
                    def _():
                        fwd_cp[kk].wait_recv()
                        in_lhs(2, kk, nxt).start()

            z = jnp.dot(lhs[ls], w[slot], preferred_element_type=F32)
            o[slot] = (z * 0.5 * (1.0 + lax.erf(z * 0.7071067811865476))).astype(BF)
            pltpu.make_async_copy(o.at[slot], h_ref.at[which, ds(k, M), ds(j, T)], o_sem.at[slot]).start()
            return 0

        lax.fori_loop(0, NU, u_step, 0)
        return 0

    lax.fori_loop(0, 8, block, 0)
    for s in (0, 1):
        pltpu.make_async_copy(o.at[s], h_ref.at[0, pl.ds(0, M), pl.ds(0, T)], o_sem.at[s]).wait()
    for cp in far_cp + sib_cp + fwd_cp:
        cp.wait_send()


def enter_call(x, gain, bias, wq, wu):
    rows, d = x.shape
    M, T = rows // 2, 1280
    cq, cu = wq.shape[0] * 128, wu.shape[1]
    dma = pltpu.SemaphoreType.DMA
    whole = pl.BlockSpec(memory_space=pltpu.VMEM)
    out = pl.pallas_call(
        functools.partial(enter_body, M=M, T=T, NQ=cq // T, NU=cu // T),
        in_specs=[ANY, whole, whole, ANY, ANY], out_specs=[ANY] * 4,
        out_shape=[jax.ShapeDtypeStruct((4, rows, cq), BF), jax.ShapeDtypeStruct((4, rows, cu), BF),
                   jax.ShapeDtypeStruct((rows, d), BF), jax.ShapeDtypeStruct((3, rows, d), BF)],
        scratch_shapes=[pltpu.VMEM((2, M, d), BF), pltpu.VMEM((2, d, T), BF), pltpu.VMEM((2, M, T), BF),
                        pltpu.VMEM((2, 128, d), BF),
                        dma((2,)), dma((2,)), dma((2,)), dma((2,)), dma((2,)), dma((6,)), dma((6,))],
        compiler_params=pltpu.CompilerParams(collective_id=0, has_side_effects=True, vmem_limit_bytes=VMEM_LIMIT),
        name="enter")(x, gain, bias, wq, wu)
    return out[0], out[1]


def attend_body(qkv_ref, o_ref, *, heads, scale):
    Q = 256
    B = Q // 128
    c = scale * 1.4426950408889634
    keep = (lax.broadcasted_iota(jnp.int32, (Q, Q), 0) <= lax.broadcasted_iota(jnp.int32, (Q, Q), 1))

    def grab(g, i, n, j):
        return qkv_ref[i:i + n, 0, :, g * 384 + j * 128:g * 384 + j * 128 + 128].reshape(n * 128, 128)

    def scores(g, i):
        return lax.dot_general(grab(g, 0, B * (i + 1), 1), grab(g, B * i, B, 0), (((1,), (1,)), ((), ())),
                               preferred_element_type=F32)

    def probs(s, i):
        tail = jnp.where(keep, s[Q * i:], -jnp.inf)
        s = tail if i == 0 else jnp.concatenate([s[:Q * i], tail], axis=0)
        p = jnp.exp2((s - jnp.max(s, axis=0, keepdims=True)) * c)
        return (p * (1.0 / jnp.sum(p, axis=0, keepdims=True))).astype(BF)

    def out(g, i, p):
        o = lax.dot_general(grab(g, 0, B * (i + 1), 2), p, (((0,), (0,)), ((), ())), preferred_element_type=F32)
        o_ref[B * i:B * i + B, 0, :, g * 128:g * 128 + 128] = o.T.astype(BF).reshape(B, 128, 128)

    ahead, behind = 3, 2
    units = [(g, i) for g in range(heads) for i in range(4 // B)]
    s = {n: scores(*units[n]) for n in range(ahead)}
    p = {}
    for n, (g, i) in enumerate(units):
        if n + ahead < len(units):
            s[n + ahead] = scores(*units[n + ahead])
        p[n] = probs(s.pop(n), i)
        if n >= behind:
            out(*units[n - behind], p.pop(n - behind))
    for n in sorted(p):
        out(*units[n], p[n])


def attend_call(qkv, heads):
    _, b, s, cq = qkv.shape
    return pl.pallas_call(
        functools.partial(attend_body, heads=heads, scale=128 ** -0.5), grid=(b,),
        in_specs=[pl.BlockSpec((4, 1, s, cq), lambda i: (0, i, 0, 0))],
        out_specs=pl.BlockSpec((4, 1, s, heads * 128), lambda i: (0, i, 0, 0)),
        out_shape=jax.ShapeDtypeStruct((4, b, s, heads * 128), BF),
        compiler_params=pltpu.CompilerParams(vmem_limit_bytes=VMEM_LIMIT), name="attend")(qkv)


def leave_body(c_ref, h_ref, wo_ref, wd_ref, x_ref, y_ref, out_ro, out_sib, out_rs, in_ro, in_sib, in_rs,
               lhs, w, stage, ra, rb, xs, l_sem, w_sem, st_sem, a_sem, s_ro, r_ro, s_rs, r_rs, s_sib, r_sib, *, M, T):
    LAG, CHUNK = 3, 384
    t, sib, far, far_sib = neighbours()
    meet(sib, far)
    kc, kh = c_ref.shape[2], h_ref.shape[2]
    N = wd_ref.shape[1] // T
    W = N // 2

    def w_copies(j, slot, width):
        cols = pl.ds(0, width)
        return (pltpu.make_async_copy(wo_ref.at[:, ds(j, width)], w.at[slot, pl.ds(0, kc), cols], w_sem.at[slot, 0]),
                pltpu.make_async_copy(wd_ref.at[:, ds(j, width)], w.at[slot, pl.ds(kc, kh), cols], w_sem.at[slot, 1]))

    pos_of = {"own": t, "sib": sib, "rs": far, "ro": far_sib}
    rel_of = {"own": 0, "sib": 1, "rs": 2, "ro": 3}

    def l_copies(kind, k, slot):
        return (pltpu.make_async_copy(c_ref.at[pos_of[kind], ds(k, M), :], lhs.at[slot, :, pl.ds(0, kc)], l_sem.at[slot, 0]),
                pltpu.make_async_copy(h_ref.at[rel_of[kind], ds(k, M), :], lhs.at[slot, :, pl.ds(kc, kh)], l_sem.at[slot, 1]))

    def start(cps):
        for cp in cps:
            cp.start()

    def wait(cps):
        for cp in cps:
            cp.wait()

    def remote(kind, i):
        src, dst, ss, rs, peer = {"ro": (out_ro, in_ro, s_ro, r_ro, sib), "sib": (out_sib, in_sib, s_sib, r_sib, sib),
                                  "rs": (out_rs, in_rs, s_rs, r_rs, far)}[kind]
        return send(src.at[i], dst.at[i], ss.at[i], rs.at[i], peer)

    def put(kind, i, slot):
        if kind == "own":
            return pltpu.make_async_copy(stage.at[slot], y_ref.at[ds(i // W, M), ds(lax.rem(i, W), 2 * T)], st_sem.at[slot])
        if kind == "sib":
            return pltpu.make_async_copy(stage.at[slot], out_sib.at[i], st_sem.at[slot])
        return pltpu.make_async_copy(stage.at[slot, :, pl.ds(0, T)], (out_ro if kind == "ro" else out_rs).at[i],
                                     st_sem.at[slot])

    def pass_on(kind, i, slot):
        put(kind, i, slot).wait()
        if kind != "own":
            remote(kind, i).start()

    def adds(kind, i, slot):
        if kind == "rs":
            return (pltpu.make_async_copy(in_ro.at[i], ra.at[slot, :, pl.ds(0, T)], a_sem.at[slot, 0]),)
        if kind == "own":
            return (pltpu.make_async_copy(in_sib.at[i], ra.at[slot], a_sem.at[slot, 0]),
                    pltpu.make_async_copy(in_rs.at[2 * i], rb.at[slot, :, pl.ds(0, T)], a_sem.at[slot, 1]),
                    pltpu.make_async_copy(in_rs.at[2 * i + 1], rb.at[slot, :, pl.ds(T, T)], a_sem.at[slot, 2]),
                    pltpu.make_async_copy(x_ref.at[ds(i // W, M), ds(lax.rem(i, W), 2 * T)], xs.at[slot], a_sem.at[slot, 3]))
        return ()

    def fetch(kind, i, slot):
        if kind == "rs":
            remote("ro", i).wait_recv()
        if kind == "own":
            remote("sib", i).wait_recv()
            remote("rs", 2 * i).wait_recv()
            remote("rs", 2 * i + 1).wait_recv()
        start(adds(kind, i, slot))
        if kind in ("ro", "rs"):
            start(w_copies(lax.rem(i, N), slot, T))
        else:
            start(w_copies(lax.rem(i, W), slot, 2 * T))

    def product(kind, i, ls, slot):
        wait(adds(kind, i, slot))
        cols = T if kind in ("ro", "rs") else 2 * T
        for r in range(0, M, CHUNK):
            rows = slice(r, r + CHUNK)
            z = jnp.dot(lhs[ls, rows], w[slot, :, 0:cols], preferred_element_type=F32)
            if kind == "rs":
                z = z + ra[slot, rows, 0:cols].astype(F32)
            if kind == "own":
                z = (z + ra[slot, rows].astype(F32)) + rb[slot, rows].astype(F32)
                z = xs[slot, rows].astype(F32) + z.astype(BF).astype(F32)
            stage[slot, rows, 0:cols] = z.astype(BF)

    fetch("ro", 0, 0)
    start(l_copies("ro", 0, 0))
    start(l_copies("rs", 0, 1))
    last = 2 * N - 1

    def far_rows(i, _):
        ro_slot = jnp.where(i < LAG, lax.rem(i, 2), LAG % 2)
        rs_slot = jnp.where(i <= last, 1 - LAG % 2, lax.rem(1 - LAG % 2 + i - last, 2))
        r = i - LAG

        @pl.when(i <= last)
        def _():
            @pl.when(lax.rem(i, N) == 0)
            def _():
                wait(l_copies("ro", 0, 0))
            wait(w_copies(0, ro_slot, T))

            @pl.when(i < LAG)
            def _():
                fetch("ro", i + 1, 1 - ro_slot)

            @pl.when(i >= LAG)
            def _():
                fetch("rs", r, 1 - ro_slot)
            product("ro", i, 0, ro_slot)

            @pl.when((i > 0) & (i <= LAG))
            def _():
                pass_on("ro", i - 1, 1 - ro_slot)

            @pl.when(i > LAG)
            def _():
                pass_on("rs", r - 1, 1 - ro_slot)
            put("ro", i, ro_slot).start()

            @pl.when(i == N - 1)
            def _():
                start(l_copies("ro", 1, 0))

        @pl.when(i >= LAG)
        def _():
            @pl.when(lax.rem(r, N) == 0)
            def _():
                wait(l_copies("rs", 0, 1))
            wait(w_copies(0, rs_slot, T))

            @pl.when(i < last)
            def _():
                fetch("ro", i + 1, 1 - rs_slot)

            @pl.when((i >= last) & (r < last))
            def _():
                fetch("rs", r + 1, 1 - rs_slot)

            @pl.when(r == last)
            def _():
                fetch("sib", 0, 1 - rs_slot)

            @pl.when(i == last)
            def _():
                start(l_copies("sib", 0, 0))
            product("rs", r, 1, rs_slot)

            @pl.when(i <= last)
            def _():
                pass_on("ro", i, 1 - rs_slot)

            @pl.when(i > last)
            def _():
                pass_on("rs", r - 1, 1 - rs_slot)
            put("rs", r, rs_slot).start()

            @pl.when(r == N - 1)
            def _():
                start(l_copies("rs", 1, 1))

            @pl.when(r == last)
            def _():
                start(l_copies("sib", 1, 1))
        return 0

    lax.fori_loop(0, last + 1 + LAG, far_rows, 0)
    end_slot = (1 - LAG % 2 + LAG) % 2
    base = 1 - end_slot

    def near_rows(kind, before):
        def step(i, _):
            k, slot = i // W, lax.rem(i + base, 2)

            @pl.when(lax.rem(i, W) == 0)
            def _():
                wait(l_copies(kind, 0, k))
            wait(w_copies(0, slot, 2 * T))

            @pl.when(i < 2 * W - 1)
            def _():
                fetch(kind, i + 1, 1 - slot)

            if kind == "sib":
                @pl.when(i == 2 * W - 1)
                def _():
                    fetch("own", 0, 1 - slot)

                @pl.when(i == W)
                def _():
                    start(l_copies("own", 0, 0))
            product(kind, i, k, slot)

            @pl.when(i == 0)
            def _():
                pass_on(before, last if before == "rs" else 2 * W - 1, 1 - slot)

            @pl.when(i > 0)
            def _():
                pass_on(kind, i - 1, 1 - slot)
            put(kind, i, slot).start()
            return 0

        lax.fori_loop(0, 2 * W, step, 0)

    near_rows("sib", "rs")
    start(l_copies("own", 1, 1))
    near_rows("own", "sib")
    put("own", 2 * W - 1, (2 * W - 1 + base) % 2).wait()

    def drain(i, _):
        remote("ro", i).wait_send()
        remote("rs", i).wait_send()

        @pl.when(i < 2 * W)
        def _():
            remote("sib", i).wait_send()
        return 0

    lax.fori_loop(0, 2 * N, drain, 0)


def leave_call(ctx, h, wo, wd, x):
    rows, d = x.shape
    M, T = rows // 2, 512
    N = d // T
    K = ctx.shape[2] + h.shape[2]
    dma = pltpu.SemaphoreType.DMA
    thin, wide = jax.ShapeDtypeStruct((2 * N, M, T), BF), jax.ShapeDtypeStruct((N, M, 2 * T), BF)
    out = pl.pallas_call(
        functools.partial(leave_body, M=M, T=T),
        in_specs=[ANY] * 5, out_specs=[ANY] * 7,
        out_shape=[jax.ShapeDtypeStruct((rows, d), BF), thin, wide, thin, thin, wide, thin],
        scratch_shapes=[pltpu.VMEM((2, M, K), BF), pltpu.VMEM((2, K, 2 * T), BF)] + [pltpu.VMEM((2, M, 2 * T), BF)] * 4
        + [dma((2, 2)), dma((2, 2)), dma((2,)), dma((2, 4))] + [dma((2 * N,))] * 4 + [dma((N,))] * 2,
        compiler_params=pltpu.CompilerParams(collective_id=1, has_side_effects=True, vmem_limit_bytes=VMEM_LIMIT),
        name="leave")(ctx, h, wo, wd, x)
    return out[0]


def solution(mesh):
    def local_layer(x_blk, ln_gain, ln_bias, w_qkv, w_out, w_up, w_down):
        b, s, d = x_blk.shape
        heads = w_qkv.shape[1]
        x = x_blk.reshape(b * s, d)
        qkv, h = enter_call(x, ln_gain.reshape(1, d), ln_bias.reshape(1, d), w_qkv.transpose(1, 2, 0, 3).reshape(heads * 3, d, 128), w_up)
        ctx = attend_call(qkv.reshape(4, b, s, -1), heads)
        y = leave_call(ctx.reshape(4, b * s, -1), h, w_out, w_down, x)
        return y.reshape(b, s, d)

    return jax.shard_map(
        local_layer, mesh=mesh,
        in_specs=(P("dp", "tp", None), P(), P(), P(None, "tp", None, None),
                  P("tp", None), P(None, "tp"), P("tp", None)),
        out_specs=P("dp", "tp", None), check_vma=False)
```

time: 2390 us -> 1100 us (0.46)
  matrix products: 1210 us -> 0 us
  Pallas kernels: 0 us -> 1080 us
  waiting for transfers between devices: 771 us -> 0 us
  other arithmetic: 388 us -> 0 us
    dot_general x6 -> x0, matrix products: 1210 us -> none  [the longest x1 387 us: local_layer(): jnp.einsum('bsd,df->bsf', normed, w_up, preferred_element_type=jnp.float32)]
    pallas_call x0 -> x3, Pallas kernels: none -> 1080 us  [the longest x1 609 us: enter_call(): pl.pallas_call(functools.partial(enter_body, M=M, T=T, NQ=cq // T, NU=cu...]
    reduce_scatter x1 -> x0, waiting for transfers between devices: 401 us -> none  [local_layer(): lax.psum_scatter(branch_part, 'tp', scatter_dimension=1, tiled=True)]
    all_gather x1 -> x0, waiting for transfers between devices: 369 us -> none  [local_layer(): x_full = lax.all_gather(x_blk, 'tp', axis=1, tiled=True)]
    dot_general x1 -> x0, other arithmetic: 287 us -> none  [local_layer(): jnp.einsum('bsf,fd->bsd', activated, w_down, preferred_element_type=jnp.f...]
    reduce_sum x3 -> x0, other arithmetic: 81.9 us -> none  [the longest x1 38.8 us: local_layer(): attn_prob = jax.nn.softmax(scores, axis=-1).astype(jnp.bfloat16)]
  transfers between devices with their start and end apart: 2 -> 0, of which waited for: 2 -> 0; matrix products, arithmetic and copies ran while one was open for 0% -> 0% of each run, Pallas kernels for 0% -> 0%
where the time goes in v2:
time: 1100 us
  Pallas kernels  1080 us (98%)
  local copies, waits for them, and re-layouts  13.2 us (1%)
    pallas_call x1, Pallas kernels, enter_call(): pl.pallas_call(functools.partial(enter_body, M=M, T=T, NQ=cq // T, NU=cu...  609 us
    pallas_call x1, Pallas kernels, leave_call(): pl.pallas_call(functools.partial(leave_body, M=M, T=T), in_specs=[ANY] *...  438 us
    pallas_call x1, Pallas kernels, attend_call(): pl.pallas_call(functools.partial(attend_body, heads=heads, scale=128 ** (...  36.5 us

profile of v2, /device:TPU:0, one launch (start us, length us, event | category | flops | bytes accessed | tf_op | source)
XLA Modules:
  0.0 1096.6 jit_solution(4651668836859902183)
XLA Ops:
  0.0 608.9 %enter.1 = (bf16[4,1536,3840]{2,1,0:T(8,128)(2,1)}, bf16[4,1536,5120]{2,1,0:T(8,128)(2,1)}, bf16[1536,5120]{1,0:T(8,128)(2,1)}, bf16[3,1536,5120]{2,1,0:T(8,128)(2,1)}) custom-call(bf16[1536,5120]{1,0:T(8,128)(2,1)} %bitcast.9, f32[1,5120]{1,0:T(1,128)} %bitcast.15, f32[1,5120]{1,0:T(1,128)} %bitcast.16, bf16[30,5120,128]{2,1,0:T(8,128)(2,1)} %bitcast.13, ...), custom_call_target="tpu_custom_call" | custom-call | tf_op jit(solution)/shard_map/enter/pallas_call | solution.py:201
  608.9 36.5 %attend.1 = bf16[4,12,128,1280]{3,2,1,0:T(8,128)(2,1)} custom-call(bf16[4,12,128,3840]{3,2,1,0:T(8,128)(2,1)} %bitcast.12), custom_call_target="tpu_custom_call" | custom-call | tf_op jit(solution)/shard_map/attend/pallas_call | solution.py:253
  645.4 438.0 %leave.1 = (bf16[1536,5120]{1,0:T(8,128)(2,1)}, bf16[20,768,512]{2,1,0:T(8,128)(2,1)}, bf16[10,768,1024]{2,1,0:T(8,128)(2,1)}, bf16[20,768,512]{2,1,0:T(8,128)(2...) custom-call(bf16[4,1536,1280]{2,1,0:T(8,128)(2,1)} %bitcast.11, ...), custom_call_target="tpu_custom_call" | custom-call | tf_op jit(solution)/shard_map/leave/pallas_call | solution.py:488
  1083.4 13.2 %copy.9 = bf16[12,128,5120]{2,1,0:T(8,128)(2,1)} copy(bf16[12,128,5120]{2,1,0:T(8,128)(2,1)} %bitcast.14) | data formatting | bytes 31457280
